TPU v7x, 128 devices: a whole 4x4x4 slice. The times are simulated.
128 devices in a mesh: pb: 16 (over z, y_hi, core), ka: 8 (over x, y_lo).
Axes of the slice: x: 4, y: 4 (y_hi: 2, y_lo: 2; y = y_hi * 2 + y_lo), z: 4, core: 2. Of those that a mesh axis runs over, the one named last changes fastest.
Arguments:
- activations: bfloat16 [4, 4096, 768], P(None, ('pb', 'ka')), may hold values from -6 to 6
- attn_gain: float32 [768], replicated, may hold values from 0.1 to 1.9
- w_qkv: bfloat16 [768, 2304], replicated, may hold values from -0.21875 to 0.21875
- w_gate: bfloat16 [768, 768], replicated, may hold values from -0.21875 to 0.21875
- w_out: bfloat16 [768, 768], replicated, may hold values from -0.21875 to 0.21875
- pair_bias: bfloat16 [16, 4096, 4096], P(None, 'pb', 'ka'), may hold values from -240 to 240
- chain_ids: int32 [4096], replicated, may hold values from 0 to 5, as said below
- binder_flag: int32 [4096], replicated, may hold values from 0 to 1, as said below
- trans_gain: float32 [768], replicated, may hold values from 0.1 to 1.9
- w_up: bfloat16 [768, 3072], replicated, may hold values from -0.21875 to 0.21875
- w_down: bfloat16 [1536, 768], replicated, may hold values from -0.15625 to 0.15625
Outputs:
- updated: bfloat16 [4, 4096, 768], P(None, ('pb', 'ka'))
Inputs may be any that keep to these rules, and one draw needn't show every extreme that they name: `chain_ids`: chain ids never fall along the tokens; every chain has at least one token. `binder_flag`: all tokens of one chain carry the same flag.
All inputs are finite; a program needn't handle non-finite values.
Results may differ from a plain program's by a relative error of at most 0.0056.
Values may be sent and summed in bfloat16 or wider, within the bound.
A program may use at most 128 MiB of HBM per device.

v0:
```python
import math
import jax
import jax.numpy as jnp
from jax import lax
from jax.sharding import PartitionSpec as P

epsilon = 1e-05
masked_score = -1000000000.0


def in_one_piece(arrays, axis, dim, along):
    ends, at = ([], 0)
    for a in arrays[:-1]:
        at += a.shape[along]
        ends.append(at)
    both = jnp.concatenate(arrays, axis=along)
    return tuple(jnp.split(lax.all_gather(both, axis, axis=dim, tiled=True), ends, axis=along))


def spread_2(value, axis, source):
    kept = jnp.where(lax.axis_index(axis) == source, value, 0).astype(value.dtype)
    return lax.psum(kept, axis)


def layer_norm(values, scales):
    centred = values - jnp.mean(values, axis=-1, keepdims=True)
    spread = jnp.mean(centred * centred, axis=-1, keepdims=True)
    return centred * lax.rsqrt(spread + epsilon) * scales


def block_stats(query_rows, key_block, value_block, bias_tile, allowed):
    head_count = bias_tile.shape[0]
    query_heads = query_rows.reshape(query_rows.shape[0], head_count, -1)
    key_heads = key_block.reshape(key_block.shape[0], head_count, -1)
    value_heads = value_block.reshape(value_block.shape[0], head_count, -1)
    head_size = query_heads.shape[-1]
    scores = jnp.einsum(
        "qhd,khd->hqk", query_heads, key_heads, preferred_element_type=jnp.float32
    ) / math.sqrt(head_size)
    scores = scores + bias_tile.astype(jnp.float32)
    best_score = jnp.max(jnp.where(allowed[None], scores, masked_score), axis=-1)
    weights = jnp.where(allowed[None], jnp.exp(scores - best_score[..., None]), 0.0)
    row_sum = jnp.sum(weights, axis=-1)
    block_out = jnp.einsum(
        "hqk,khd->qhd",
        weights.astype(jnp.bfloat16),
        value_heads,
        preferred_element_type=jnp.float32,
    )
    return (best_score.T, row_sum.T, block_out.reshape(query_rows.shape[0], -1))


def body(
    activations,
    attn_gain,
    w_qkv,
    w_gate,
    w_out,
    pair_bias,
    chain_ids,
    binder_flag,
    trans_gain,
    w_up,
    w_down,
):
    samples, own_rows, model_width = activations.shape
    head_count, query_count, key_count = pair_bias.shape
    pb_ratio = lax.axis_size("pb") // lax.axis_size("ka")
    normed = layer_norm(activations.astype(jnp.float32), attn_gain).astype(jnp.bfloat16)
    flat_normed = normed.reshape(-1, model_width)
    gate_pre = jnp.dot(flat_normed, w_gate, preferred_element_type=jnp.float32).reshape(
        samples, own_rows, model_width
    )
    queries = jnp.dot(flat_normed, w_qkv[:, :model_width], preferred_element_type=jnp.float32)
    queries = queries.astype(jnp.bfloat16).reshape(samples, own_rows, model_width)
    queries, block_normed = in_one_piece((queries, normed), "ka", 1, 0)
    input_parts = []
    for within in range(pb_ratio):
        source_index = lax.axis_index("ka") * pb_ratio + within
        input_parts.append(spread_2(block_normed, "pb", source_index))
    key_inputs = jnp.concatenate(input_parts, axis=1).reshape(-1, model_width)
    key_value = jnp.dot(key_inputs, w_qkv[:, model_width:], preferred_element_type=jnp.float32)
    key_block = (
        key_value[:, :model_width].astype(jnp.bfloat16).reshape(samples, key_count, model_width)
    )
    value_block = (
        key_value[:, model_width:].astype(jnp.bfloat16).reshape(samples, key_count, model_width)
    )
    query_start = lax.axis_index("pb") * query_count
    key_start = lax.axis_index("ka") * key_count
    row_chain = lax.dynamic_slice_in_dim(chain_ids, query_start, query_count, 0)
    row_binder = lax.dynamic_slice_in_dim(binder_flag, query_start, query_count, 0)
    col_chain = lax.dynamic_slice_in_dim(chain_ids, key_start, key_count, 0)
    col_binder = lax.dynamic_slice_in_dim(binder_flag, key_start, key_count, 0)
    allowed = (
        (row_binder[:, None] > 0)
        | (col_binder[None, :] > 0)
        | (row_chain[:, None] == col_chain[None, :])
    )

    def per_sample(operands):
        return block_stats(operands[0], operands[1], operands[2], pair_bias, allowed)

    block_tops, block_sums, block_outs = lax.map(per_sample, (queries, key_block, value_block))
    all_tops, all_sums, all_outs = (
        lax.all_to_all(block_tops[None], "ka", split_axis=2, concat_axis=0, tiled=True),
        lax.all_to_all(block_sums[None], "ka", split_axis=2, concat_axis=0, tiled=True),
        lax.all_to_all(block_outs[None], "ka", split_axis=2, concat_axis=0, tiled=True),
    )
    overall = jnp.max(all_tops, axis=0)
    factors = jnp.exp(all_tops - overall)
    row_sum = jnp.sum(factors * all_sums, axis=0)
    shaped = all_outs.reshape(all_outs.shape[:-1] + (head_count, -1))
    row_out = jnp.sum(factors[..., None] * shaped, axis=0).reshape(samples, own_rows, model_width)
    attention = (row_out.reshape(samples, own_rows, head_count, -1) / row_sum[..., None]).reshape(
        samples, own_rows, model_width
    )
    gated = (jax.nn.sigmoid(gate_pre) * attention).astype(jnp.bfloat16)
    mixed = activations.astype(jnp.float32) + jnp.dot(
        gated.reshape(-1, model_width), w_out, preferred_element_type=jnp.float32
    ).reshape(samples, own_rows, model_width)
    trans_normed = layer_norm(mixed, trans_gain).astype(jnp.bfloat16)
    both_parts = jnp.dot(
        trans_normed.reshape(-1, model_width), w_up, preferred_element_type=jnp.float32
    )
    hidden_width = w_down.shape[0]
    hidden = (jax.nn.silu(both_parts[:, :hidden_width]) * both_parts[:, hidden_width:]).astype(
        jnp.bfloat16
    )
    updated = mixed + jnp.dot(hidden, w_down, preferred_element_type=jnp.float32).reshape(
        samples, own_rows, model_width
    )
    return updated.astype(jnp.bfloat16)


def solution(mesh):
    placed = (
        P(None, ("pb", "ka"), None),
        P(),
        P(),
        P(),
        P(),
        P(None, "pb", "ka"),
        P(),
        P(),
        P(),
        P(),
        P(),
    )
    return jax.shard_map(
        body, mesh=mesh, in_specs=placed, out_specs=P(None, ("pb", "ka"), None), check_vma=False
    )
```

profile of v0, /device:TPU:121, one launch (start us, length us, event | category | flops | bytes accessed | tf_op | source)
XLA Modules:
  0.0 497.9 jit_solution(10470582669954090714)
XLA Ops:
  12.4 70.0 %all-gather.2.cloned.1.call-done = bf16[8,256,768]{2,1,0:T(8,128)(2,1)} async-done(((bf16[8,32,768]{2,1,0:T(8,128)(2,1)}), bf16[8,256,768]{2,1,0:T(8,128)(2,1)}) %all-gather.2.cloned.1.call-update) | async-done | bytes 3145744 | tf_op jit(solution)/shard_map/all_gather | solution.py:17
  82.5 4.2 broadcast_select_fusion.1
  89.7 150.4 %all-reduce.3.cloned.1.call-done = (bf16[4,256,768]{2,1,0:T(8,128)(2,1)}, bf16[4,256,768]{2,1,0:T(8,128)(2,1)}) async-done(((bf16[4,256,768]{2,1,0:T(8,128)(2,1)}, bf16[4,256,768]{2,1,0:T(8,128)(2,1)}), (bf16[4,256,768]{2,1,0:T(8,128)(2,1)}, bf16[4,256,768]{2,1,0:T(8,128)(2,1)})) %all-reduce.3.cloned.1.call-update) | async-done | bytes 3145744 | tf_op jit(solution)/shard_map/psum | solution.py:22
  243.1 5.4 %convolution_convert_fusion = bf16[2048,1536]{1,0:T(8,128)(2,1)S(1)} fusion(bf16[2048,768]{1,0:T(8,128)(2,1)S(1)} %bitcast.103, bf16[768,2304]{1,0:T(8,128)(2,1)S(1)} %copy-done.6), kind=kOutput, calls=%fused_computation.17 | convolution fusion | flops 4834983936 | bytes 11796480 | tf_op jit(solution)/shard_map/dot_general | solution.py:82
  248.5 3.1 fusion.45
  251.6 158.6 %while.15 = (s32[]{:T(128)}, f32[4,256,16]{1,2,0:T(8,128)S(1)}, f32[4,256,16]{1,2,0:T(8,128)S(1)}, f32[4,256,768]{2,0,1:T(4,128)}, bf16[4,256,768]{2,1,0:T(8,128...) while((s32[]{:T(128)}, f32[4,256,16]{1,2,0:T(8,128)S(1)}, ...), condition=%wide.region_7.8_spmd.clone, body=%wide.region_4.7_spmd.clone.sunk | while | flops 426106880 | bytes 77336504 | solution.py:104
  256.1 4.9 select_reduce_fusion.2
  261.0 2.4 fusion.70
  267.7 5.8 %fusion.71 = f32[16,48,256]{2,1,0:T(8,128)} fusion(bf16[512,16,48]{0,2,1:T(8,128)(2,1)S(1)} %bitcast.95, f32[16,256,512]{2,1,0:T(8,128)} %copy-done.1, f32[16,256]{1,0:T(8,128)S(1)} %get-tuple-element.240, pred[256,512]{1,0:T(8,128)(4,1)S(1)} %compare_or_fusion.2), kind=kOutput, calls=%fused_computation.6.clone.1 | convolution fusion | flops 207618048 | bytes 10108928 | tf_op jit(solution)/shard_map/while/body/eval_jaxpr/hqk,khd->qhd/dot_general | solution.py:44
  275.8 15.4 %dynamic_update_slice.19 = f32[4,256,768]{2,0,1:T(4,128)} dynamic-update-slice(f32[4,256,768]{2,0,1:T(4,128)} %get-tuple-element.260, f32[1,256,768]{2,0,1:T(1,128)S(1)} %copy.49, s32[]{:T(128)S(6)} %copy.59, s32[]{:T(128)} %constant.36.clone.1..sunk, s32[]{:T(128)} %constant.36.clone.1..sunk) | dynamic-update-slice | bytes 1572868 | tf_op jit(solution)/shard_map/while/body/jit(dynamic_update_index_in_dim)/dynamic_update_slice | solution.py:104
  295.7 4.9 select_reduce_fusion.2
  300.6 2.4 fusion.70
  307.3 5.8 %fusion.71 = f32[16,48,256]{2,1,0:T(8,128)} fusion(bf16[512,16,48]{0,2,1:T(8,128)(2,1)S(1)} %bitcast.95, f32[16,256,512]{2,1,0:T(8,128)} %copy-done.1, f32[16,256]{1,0:T(8,128)S(1)} %get-tuple-element.240, pred[256,512]{1,0:T(8,128)(4,1)S(1)} %compare_or_fusion.2), kind=kOutput, calls=%fused_computation.6.clone.1 | convolution fusion | flops 207618048 | bytes 10108928 | tf_op jit(solution)/shard_map/while/body/eval_jaxpr/hqk,khd->qhd/dot_general | solution.py:44
  315.5 15.4 %dynamic_update_slice.19 = f32[4,256,768]{2,0,1:T(4,128)} dynamic-update-slice(f32[4,256,768]{2,0,1:T(4,128)} %get-tuple-element.260, f32[1,256,768]{2,0,1:T(1,128)S(1)} %copy.49, s32[]{:T(128)S(6)} %copy.59, s32[]{:T(128)} %constant.36.clone.1..sunk, s32[]{:T(128)} %constant.36.clone.1..sunk) | dynamic-update-slice | bytes 1572868 | tf_op jit(solution)/shard_map/while/body/jit(dynamic_update_index_in_dim)/dynamic_update_slice | solution.py:104
  335.4 4.9 select_reduce_fusion.2
  340.3 2.4 fusion.70
  347.0 5.8 %fusion.71 = f32[16,48,256]{2,1,0:T(8,128)} fusion(bf16[512,16,48]{0,2,1:T(8,128)(2,1)S(1)} %bitcast.95, f32[16,256,512]{2,1,0:T(8,128)} %copy-done.1, f32[16,256]{1,0:T(8,128)S(1)} %get-tuple-element.240, pred[256,512]{1,0:T(8,128)(4,1)S(1)} %compare_or_fusion.2), kind=kOutput, calls=%fused_computation.6.clone.1 | convolution fusion | flops 207618048 | bytes 10108928 | tf_op jit(solution)/shard_map/while/body/eval_jaxpr/hqk,khd->qhd/dot_general | solution.py:44
  355.1 15.4 %dynamic_update_slice.19 = f32[4,256,768]{2,0,1:T(4,128)} dynamic-update-slice(f32[4,256,768]{2,0,1:T(4,128)} %get-tuple-element.260, f32[1,256,768]{2,0,1:T(1,128)S(1)} %copy.49, s32[]{:T(128)S(6)} %copy.59, s32[]{:T(128)} %constant.36.clone.1..sunk, s32[]{:T(128)} %constant.36.clone.1..sunk) | dynamic-update-slice | bytes 1572868 | tf_op jit(solution)/shard_map/while/body/jit(dynamic_update_index_in_dim)/dynamic_update_slice | solution.py:104
  375.1 4.9 select_reduce_fusion.2
  379.9 2.4 fusion.70
  386.7 5.8 %fusion.71 = f32[16,48,256]{2,1,0:T(8,128)} fusion(bf16[512,16,48]{0,2,1:T(8,128)(2,1)S(1)} %bitcast.95, f32[16,256,512]{2,1,0:T(8,128)} %copy-done.1, f32[16,256]{1,0:T(8,128)S(1)} %get-tuple-element.240, pred[256,512]{1,0:T(8,128)(4,1)S(1)} %compare_or_fusion.2), kind=kOutput, calls=%fused_computation.6.clone.1 | convolution fusion | flops 207618048 | bytes 10108928 | tf_op jit(solution)/shard_map/while/body/eval_jaxpr/hqk,khd->qhd/dot_general | solution.py:44
  394.8 15.4 %dynamic_update_slice.19 = f32[4,256,768]{2,0,1:T(4,128)} dynamic-update-slice(f32[4,256,768]{2,0,1:T(4,128)} %get-tuple-element.260, f32[1,256,768]{2,0,1:T(1,128)S(1)} %copy.49, s32[]{:T(128)S(6)} %copy.59, s32[]{:T(128)} %constant.36.clone.1..sunk, s32[]{:T(128)} %constant.36.clone.1..sunk) | dynamic-update-slice | bytes 1572868 | tf_op jit(solution)/shard_map/while/body/jit(dynamic_update_index_in_dim)/dynamic_update_slice | solution.py:104
  411.6 5.2 %all-to-all-start.2 = ((f32[8,1,2048]{2,1,0:T(1,128)}), f32[8,1,2048]{2,1,0:T(1,128)S(1)}, u32[]{:S(2)}, u32[]{:S(2)}) async-start(f32[8,1,2048]{2,1,0:T(1,128)} %reshape.108), calls=%async_computation.2 | async-start | bytes 131072 | tf_op jit(solution)/shard_map/all_to_all | solution.py:107
  417.5 3.5 all-to-all-done.2
  420.9 7.7 %all_to_all.51 = f32[8,1,2048]{2,1,0:T(1,128)S(1)} all-to-all(f32[8,1,2048]{2,1,0:T(1,128)S(1)} %reshape.106), channel_id=1, replica_groups=mesh['pb'=16,'ka'=8] {'ka'}, dimensions={0} | all-to-all | bytes 131072 | tf_op jit(solution)/shard_map/all_to_all | solution.py:106
  428.6 5.3 %all-to-all-start.1 = ((f32[1,4,256,768]{3,1,0,2:T(4,128)}), f32[1,4,256,768]{3,1,0,2:T(4,128)}, u32[]{:S(2)}, u32[]{:S(2)}) async-start(f32[1,4,256,768]{3,1,0,2:T(4,128)} %bitcast.102), calls=%async_computation.1 | async-start | bytes 6291456 | tf_op jit(solution)/shard_map/all_to_all | solution.py:108
  437.7 4.6 mul.80
  442.2 7.7 %mul.81 = f32[8,1,4,32,768]{4,3,0,2,1:T(8,128)} reshape(f32[8,4,32,16,48]{4,3,2,0,1:T(8,128)} %mul.80) | data formatting | bytes 6291456 | tf_op jit(solution)/shard_map/mul | solution.py:114
  451.5 28.4 %all-to-all-done.1 = f32[1,4,256,768]{3,1,0,2:T(4,128)} async-done(((f32[1,4,256,768]{3,1,0,2:T(4,128)}), f32[1,4,256,768]{3,1,0,2:T(4,128)}, u32[]{:S(2)}, u32[]{:S(2)}) %all-to-all-start.1) | async-done | bytes 3145760 | tf_op jit(solution)/shard_map/all_to_all | solution.py:108
  479.9 2.6 copy.27
  483.7 2.5 fusion.46
  486.6 3.1 fusion.51
  (101 shorter events, 66.3 us)
Async XLA Ops:
  6.5 483.2 %copy-start = (bf16[1536,768]{1,0:T(8,128)(2,1)S(1)}, bf16[1536,768]{1,0:T(8,128)(2,1)}, u32[]{:S(2)}) copy-start(bf16[1536,768]{1,0:T(8,128)(2,1)} %param.23) | copy-start | bytes 7077892
  6.5 75.9 %all-gather.2.cloned.1.call-start = ((), (), s32[]{:S(2)}) async-start(), calls=%async_computation.3 | async-start | bytes 3538944 | tf_op jit(solution)/shard_map/all_gather | solution.py:17
  12.4 227.8 %all-reduce.3.cloned.1.call-start = ((), (), s32[]{:S(2)}) async-start(), calls=%async_computation.4 | async-start | bytes 6291456 | tf_op jit(solution)/shard_map/psum | solution.py:22
  240.2 2.9 copy-start.6
  261.0 3.2 copy-start.1
  300.6 3.2 copy-start.1
  340.3 3.2 copy-start.1
  379.9 3.2 copy-start.1
  411.6 9.3 %all-to-all-start.2 = ((f32[8,1,2048]{2,1,0:T(1,128)}), f32[8,1,2048]{2,1,0:T(1,128)S(1)}, u32[]{:S(2)}, u32[]{:S(2)}) async-start(f32[8,1,2048]{2,1,0:T(1,128)} %reshape.108), calls=%async_computation.2 | async-start | bytes 131072 | tf_op jit(solution)/shard_map/all_to_all | solution.py:107
  428.6 51.3 %all-to-all-start.1 = ((f32[1,4,256,768]{3,1,0,2:T(4,128)}), f32[1,4,256,768]{3,1,0,2:T(4,128)}, u32[]{:S(2)}, u32[]{:S(2)}) async-start(f32[1,4,256,768]{3,1,0,2:T(4,128)} %bitcast.102), calls=%async_computation.1 | async-start | bytes 6291456 | tf_op jit(solution)/shard_map/all_to_all | solution.py:108
  479.9 2.8 copy-start.2
  482.8 0.9 copy-start.3
  482.8 0.9 copy-start.4
  483.7 2.8 copy-start.5
Sparse Core Ops, SparseCore 0:
  12.5 69.9 all-gather.1
  86.8 153.3 all-reduce.2
where the time goes:
time: 501 us; the launch traced here: 498 us
  waiting for transfers between devices  252 us (50%)
  local copies, waits for them, and re-layouts  132 us (26%)
  matrix products  56.1 us (11%)
  other arithmetic  25.7 us (5%)
  between operations  13.7 us (3%)
  starting transfers between devices  10.5 us (2%)
  blocking collectives  7.65 us (2%)
    psum x1, waiting for transfers between devices, spread_2(): return lax.psum(kept, axis)  150 us
    dynamic_update_slice x12, local copies, waits for them, and re-layouts, body(): lax.map(per_sample, (queries, key_block, value_block))  71 us
    all_gather x1, waiting for transfers between devices, in_one_piece(): lax.all_gather(both, axis, axis=dim, tiled=True)  70 us
    dynamic_slice x24, local copies, waits for them, and re-layouts, body(): lax.map(per_sample, (queries, key_block, value_block))  31.1 us
    all_to_all x1, waiting for transfers between devices, body(): lax.all_to_all(block_outs[None], 'ka', split_axis=2, concat_axis=0, tiled...  28.4 us
    dot_general x4, matrix products, block_stats(): jnp.einsum('hqk,khd->qhd', weights.astype(jnp.bfloat16), value_heads, pre...  23.3 us
    dot_general x4, matrix products, block_stats(): jnp.einsum('qhd,khd->hqk', query_heads, key_heads, preferred_element_type...  19.5 us
    mul x2, local copies, waits for them, and re-layouts, body(): factors[..., None] * shaped  12.3 us
  transfers between devices with their start and end apart: 4, of which 4 were waited for; matrix products, arithmetic and copies ran while one was open for 4% of the time, Pallas kernels for 0%

commit v1 on v0

--- a/solution.py
+++ b/solution.py
@@ -105,7 +105,12 @@
     all_tops, all_sums, all_outs = (
         lax.all_to_all(block_tops[None], "ka", split_axis=2, concat_axis=0, tiled=True),
         lax.all_to_all(block_sums[None], "ka", split_axis=2, concat_axis=0, tiled=True),
-        lax.all_to_all(block_outs[None], "ka", split_axis=2, concat_axis=0, tiled=True),
+        jnp.concatenate(
+            lax.all_to_all(
+                jnp.stack(jnp.split(block_outs[None], lax.axis_size("ka"), axis=2)), "ka", 0, 0
+            ),
+            axis=0,
+        ),
     )
     overall = jnp.max(all_tops, axis=0)
     factors = jnp.exp(all_tops - overall)

time: 501 us -> 444 us (0.89)
  local copies, waits for them, and re-layouts: 132 us -> 78.5 us
  blocking collectives: 7.65 us -> 0 us
  starting transfers between devices: 10.5 us -> 15.8 us
    dynamic_update_slice x12, local copies, waits for them, and re-layouts: 71 us -> 9.39 us  [body(): lax.map(per_sample, (queries, key_block, value_block))]
    unnamed x18 -> x25, local copies, waits for them, and re-layouts: 3.55 us -> 12.3 us
    all_to_all x1 -> x0, blocking collectives: 7.65 us -> none  [body(): lax.all_to_all(block_tops[None], 'ka', split_axis=2, concat_axis=0, tiled...]
    all_to_all x1 -> x2, starting transfers between devices: 5.28 us -> 10.6 us  [the longest x1 5.32 us: body(): lax.all_to_all(block_tops[None], 'ka', split_axis=2, concat_axis=0, tiled...]
    all_to_all x1 -> x2, waiting for transfers between devices: 28.4 us -> 29.5 us  [the longest x1 27.1 us: body(): lax.all_to_all(jnp.stack(jnp.split(block_outs[None], lax.axis_size('ka'),...]
  transfers between devices with their start and end apart: 4 -> 5, of which waited for: 4 -> 4; matrix products, arithmetic and copies ran while one was open for 4% -> 7% of each run, Pallas kernels for 0% -> 0%
where the time goes in v1:
time: 444 us; the launch traced here: 443 us
  waiting for transfers between devices  250 us (56%)
  local copies, waits for them, and re-layouts  78.5 us (18%)
  matrix products  56.1 us (13%)
  other arithmetic  28.4 us (6%)
  starting transfers between devices  15.8 us (4%)
  between operations  13.7 us (3%)
    psum x1, waiting for transfers between devices, spread_2(): return lax.psum(kept, axis)  150 us
    all_gather x1, waiting for transfers between devices, in_one_piece(): lax.all_gather(both, axis, axis=dim, tiled=True)  70 us
    dynamic_slice x24, local copies, waits for them, and re-layouts, body(): lax.map(per_sample, (queries, key_block, value_block))  31.2 us
    all_to_all x1, waiting for transfers between devices, body(): lax.all_to_all(jnp.stack(jnp.split(block_outs[None], lax.axis_size('ka'),...  27.1 us
    dot_general x4, matrix products, block_stats(): jnp.einsum('hqk,khd->qhd', weights.astype(jnp.bfloat16), value_heads, pre...  23.3 us
    dot_general x4, matrix products, block_stats(): jnp.einsum('qhd,khd->hqk', query_heads, key_heads, preferred_element_type...  19.5 us
    mul x2, local copies, waits for them, and re-layouts, body(): factors[..., None] * shaped  12.3 us
    unnamed x25, local copies, waits for them, and re-layouts  12.3 us
  transfers between devices with their start and end apart: 5, of which 4 were waited for; matrix products, arithmetic and copies ran while one was open for 7% of the time, Pallas kernels for 0%

profile of v1, /device:TPU:121, one launch (start us, length us, event | category | flops | bytes accessed | tf_op | source)
XLA Modules:
  0.0 442.6 jit_solution(17811978237152378318)
XLA Ops:
  12.4 70.0 %all-gather.2.cloned.1.call-done = bf16[8,256,768]{2,1,0:T(8,128)(2,1)} async-done(((bf16[8,32,768]{2,1,0:T(8,128)(2,1)}), bf16[8,256,768]{2,1,0:T(8,128)(2,1)}) %all-gather.2.cloned.1.call-update) | async-done | bytes 3145744 | tf_op jit(solution)/shard_map/all_gather | solution.py:17
  82.5 4.2 broadcast_select_fusion.1
  89.8 150.4 %all-reduce.3.cloned.1.call-done = (bf16[4,256,768]{2,1,0:T(8,128)(2,1)}, bf16[4,256,768]{2,1,0:T(8,128)(2,1)}) async-done(((bf16[4,256,768]{2,1,0:T(8,128)(2,1)}, bf16[4,256,768]{2,1,0:T(8,128)(2,1)}), (bf16[4,256,768]{2,1,0:T(8,128)(2,1)}, bf16[4,256,768]{2,1,0:T(8,128)(2,1)})) %all-reduce.3.cloned.1.call-update) | async-done | bytes 3145744 | tf_op jit(solution)/shard_map/psum | solution.py:22
  240.2 2.2 pad_maximum_fusion
  243.1 5.4 %convolution_convert_fusion = bf16[2048,1536]{1,0:T(8,128)(2,1)S(1)} fusion(bf16[2048,768]{1,0:T(8,128)(2,1)S(1)} %bitcast.136, bf16[768,2304]{1,0:T(8,128)(2,1)S(1)} %copy-done.6), kind=kOutput, calls=%fused_computation.18 | convolution fusion | flops 4834983936 | bytes 11796480 | tf_op jit(solution)/shard_map/dot_general | solution.py:82
  248.5 3.1 fusion.53
  251.6 97.4 %while.15 = (s32[]{:T(128)}, f32[4,256,16]{1,2,0:T(8,128)S(1)}, f32[4,256,16]{1,2,0:T(8,128)S(1)}, f32[4,256,768]{2,1,0:T(8,128)}, bf16[4,256,768]{2,1,0:T(8,128...) while((s32[]{:T(128)}, f32[4,256,16]{1,2,0:T(8,128)S(1)}, ...), condition=%wide.region_7.8_spmd.clone, body=%wide.region_4.7_spmd.clone.sunk | while | flops 426106880 | bytes 77336496 | solution.py:104
  256.1 4.9 %select_reduce_fusion.2 = (f32[16,256]{1,0:T(8,128)S(1)}, f32[16,256,512]{2,1,0:T(8,128)S(1)}) fusion(pred[256,512]{1,0:T(8,128)(4,1)S(1)} %compare_or_fusion.2, bf16[16,256,512]{2,1,0:T(8,128)(2,1)} %get-tuple-element.275, bf16[256,16,48]{0,2,1:T(8,128)(2,1)} %bitcast.125, bf16[512,16,48]{0,2,1:T(8,128)(2,1)} %bitcast.124), kind=kOutput, calls=%fused_computation.2.clone.1 | convolution fusion | flops 211808256 | bytes 13910016 | tf_op jit(solution)/shard_map/while/body/eval_jaxpr/qhd,khd->hqk/dot_general | solution.py:37
  261.0 2.4 fusion.78
  264.3 2.1 constant_dynamic-slice_fusion.8
  267.8 5.8 %fusion.79 = f32[16,48,256]{2,1,0:T(8,128)} fusion(bf16[512,16,48]{0,2,1:T(8,128)(2,1)S(1)} %bitcast.122, f32[16,256,512]{2,1,0:T(8,128)} %copy-done.1, f32[16,256]{1,0:T(8,128)S(1)} %get-tuple-element.240, pred[256,512]{1,0:T(8,128)(4,1)S(1)} %compare_or_fusion.2), kind=kOutput, calls=%fused_computation.6.clone.1 | convolution fusion | flops 207618048 | bytes 10108928 | tf_op jit(solution)/shard_map/while/body/eval_jaxpr/hqk,khd->qhd/dot_general | solution.py:44
  280.4 4.9 %select_reduce_fusion.2 = (f32[16,256]{1,0:T(8,128)S(1)}, f32[16,256,512]{2,1,0:T(8,128)S(1)}) fusion(pred[256,512]{1,0:T(8,128)(4,1)S(1)} %compare_or_fusion.2, bf16[16,256,512]{2,1,0:T(8,128)(2,1)} %get-tuple-element.275, bf16[256,16,48]{0,2,1:T(8,128)(2,1)} %bitcast.125, bf16[512,16,48]{0,2,1:T(8,128)(2,1)} %bitcast.124), kind=kOutput, calls=%fused_computation.2.clone.1 | convolution fusion | flops 211808256 | bytes 13910016 | tf_op jit(solution)/shard_map/while/body/eval_jaxpr/qhd,khd->hqk/dot_general | solution.py:37
  285.3 2.4 fusion.78
  288.6 2.1 constant_dynamic-slice_fusion.8
  292.1 5.8 %fusion.79 = f32[16,48,256]{2,1,0:T(8,128)} fusion(bf16[512,16,48]{0,2,1:T(8,128)(2,1)S(1)} %bitcast.122, f32[16,256,512]{2,1,0:T(8,128)} %copy-done.1, f32[16,256]{1,0:T(8,128)S(1)} %get-tuple-element.240, pred[256,512]{1,0:T(8,128)(4,1)S(1)} %compare_or_fusion.2), kind=kOutput, calls=%fused_computation.6.clone.1 | convolution fusion | flops 207618048 | bytes 10108928 | tf_op jit(solution)/shard_map/while/body/eval_jaxpr/hqk,khd->qhd/dot_general | solution.py:44
  304.8 4.9 %select_reduce_fusion.2 = (f32[16,256]{1,0:T(8,128)S(1)}, f32[16,256,512]{2,1,0:T(8,128)S(1)}) fusion(pred[256,512]{1,0:T(8,128)(4,1)S(1)} %compare_or_fusion.2, bf16[16,256,512]{2,1,0:T(8,128)(2,1)} %get-tuple-element.275, bf16[256,16,48]{0,2,1:T(8,128)(2,1)} %bitcast.125, bf16[512,16,48]{0,2,1:T(8,128)(2,1)} %bitcast.124), kind=kOutput, calls=%fused_computation.2.clone.1 | convolution fusion | flops 211808256 | bytes 13910016 | tf_op jit(solution)/shard_map/while/body/eval_jaxpr/qhd,khd->hqk/dot_general | solution.py:37
  309.7 2.4 fusion.78
  313.0 2.1 constant_dynamic-slice_fusion.8
  316.5 5.8 %fusion.79 = f32[16,48,256]{2,1,0:T(8,128)} fusion(bf16[512,16,48]{0,2,1:T(8,128)(2,1)S(1)} %bitcast.122, f32[16,256,512]{2,1,0:T(8,128)} %copy-done.1, f32[16,256]{1,0:T(8,128)S(1)} %get-tuple-element.240, pred[256,512]{1,0:T(8,128)(4,1)S(1)} %compare_or_fusion.2), kind=kOutput, calls=%fused_computation.6.clone.1 | convolution fusion | flops 207618048 | bytes 10108928 | tf_op jit(solution)/shard_map/while/body/eval_jaxpr/hqk,khd->qhd/dot_general | solution.py:44
  329.2 4.9 %select_reduce_fusion.2 = (f32[16,256]{1,0:T(8,128)S(1)}, f32[16,256,512]{2,1,0:T(8,128)S(1)}) fusion(pred[256,512]{1,0:T(8,128)(4,1)S(1)} %compare_or_fusion.2, bf16[16,256,512]{2,1,0:T(8,128)(2,1)} %get-tuple-element.275, bf16[256,16,48]{0,2,1:T(8,128)(2,1)} %bitcast.125, bf16[512,16,48]{0,2,1:T(8,128)(2,1)} %bitcast.124), kind=kOutput, calls=%fused_computation.2.clone.1 | convolution fusion | flops 211808256 | bytes 13910016 | tf_op jit(solution)/shard_map/while/body/eval_jaxpr/qhd,khd->hqk/dot_general | solution.py:37
  334.0 2.4 fusion.78
  340.8 5.8 %fusion.79 = f32[16,48,256]{2,1,0:T(8,128)} fusion(bf16[512,16,48]{0,2,1:T(8,128)(2,1)S(1)} %bitcast.122, f32[16,256,512]{2,1,0:T(8,128)} %copy-done.1, f32[16,256]{1,0:T(8,128)S(1)} %get-tuple-element.240, pred[256,512]{1,0:T(8,128)(4,1)S(1)} %compare_or_fusion.2), kind=kOutput, calls=%fused_computation.6.clone.1 | convolution fusion | flops 207618048 | bytes 10108928 | tf_op jit(solution)/shard_map/while/body/eval_jaxpr/hqk,khd->qhd/dot_general | solution.py:44
  350.4 5.2 %all-to-all-start.2 = ((f32[8,1,2048]{2,1,0:T(1,128)}), f32[8,1,2048]{2,1,0:T(1,128)S(1)}, u32[]{:S(2)}, u32[]{:S(2)}) async-start(f32[8,1,2048]{2,1,0:T(1,128)} %reshape.106), calls=%async_computation.2 | async-start | bytes 131072 | tf_op jit(solution)/shard_map/all_to_all | solution.py:107
  365.5 5.3 %all-to-all-start = ((f32[8,1,2048]{2,1,0:T(1,128)}), f32[8,1,2048]{2,1,0:T(1,128)S(1)}, u32[]{:S(2)}, u32[]{:S(2)}) async-start(f32[8,1,2048]{2,1,0:T(1,128)} %reshape.104), calls=%async_computation | async-start | bytes 131072 | tf_op jit(solution)/shard_map/all_to_all | solution.py:106
  372.6 2.4 all-to-all-done
  375.0 5.2 %all-to-all-start.1 = ((f32[8,1,4,32,768]{4,3,2,1,0:T(8,128)}), f32[8,1,4,32,768]{4,3,2,1,0:T(8,128)}, u32[]{:S(2)}, u32[]{:S(2)}) async-start(f32[8,1,4,32,768]{4,3,2,1,0:T(8,128)} %fusion.35), calls=%async_computation.1 | async-start | bytes 6291456 | tf_op jit(solution)/shard_map/all_to_all | solution.py:109
  384.0 4.6 %mul.80 = f32[8,4,32,16,48]{4,3,2,1,0:T(8,128)} broadcast(f32[8,4,32,16]{3,2,1,0:T(8,128)S(1)} %copy.32), dimensions={0,1,2,3} | broadcast | bytes 3211264 | tf_op jit(solution)/shard_map/mul | solution.py:119
  388.6 7.7 %mul.81 = f32[8,1,4,32,768]{4,3,2,1,0:T(8,128)} reshape(f32[8,4,32,16,48]{4,3,2,1,0:T(8,128)} %mul.80) | data formatting | bytes 6291456 | tf_op jit(solution)/shard_map/mul | solution.py:119
  398.0 27.1 %all-to-all-done.1 = f32[8,1,4,32,768]{4,3,2,1,0:T(8,128)} async-done(((f32[8,1,4,32,768]{4,3,2,1,0:T(8,128)}), f32[8,1,4,32,768]{4,3,2,1,0:T(8,128)}, u32[]{:S(2)}, u32[]{:S(2)}) %all-to-all-start.1) | async-done | bytes 3145760 | tf_op jit(solution)/shard_map/all_to_all | solution.py:109
  425.1 3.3 multiply_reduce_fusion
  428.4 2.5 fusion.54
  431.3 3.2 fusion.59
  (109 shorter events, 68.3 us)
Async XLA Ops:
  6.5 427.9 %copy-start = (bf16[1536,768]{1,0:T(8,128)(2,1)S(1)}, bf16[1536,768]{1,0:T(8,128)(2,1)}, u32[]{:S(2)}) copy-start(bf16[1536,768]{1,0:T(8,128)(2,1)} %param.23) | copy-start | bytes 7077892
  6.5 75.9 %all-gather.2.cloned.1.call-start = ((), (), s32[]{:S(2)}) async-start(), calls=%async_computation.3 | async-start | bytes 3538944 | tf_op jit(solution)/shard_map/all_gather | solution.py:17
  12.4 227.8 %all-reduce.3.cloned.1.call-start = ((), (), s32[]{:S(2)}) async-start(), calls=%async_computation.4 | async-start | bytes 6291456 | tf_op jit(solution)/shard_map/psum | solution.py:22
  240.2 2.9 copy-start.6
  261.0 3.3 copy-start.1
  285.3 3.3 copy-start.1
  309.7 3.3 copy-start.1
  334.0 3.3 copy-start.1
  350.4 15.1 %all-to-all-start.2 = ((f32[8,1,2048]{2,1,0:T(1,128)}), f32[8,1,2048]{2,1,0:T(1,128)S(1)}, u32[]{:S(2)}, u32[]{:S(2)}) async-start(f32[8,1,2048]{2,1,0:T(1,128)} %reshape.106), calls=%async_computation.2 | async-start | bytes 131072 | tf_op jit(solution)/shard_map/all_to_all | solution.py:107
  355.8 5.5 %copy-start.2 = (f32[4,256,768]{2,1,0:T(8,128)S(1)}, f32[4,256,768]{2,1,0:T(8,128)}, u32[]{:S(2)}) copy-start(f32[4,256,768]{2,1,0:T(8,128)} %get-tuple-element.55) | copy-start | bytes 9437188
  365.5 9.5 %all-to-all-start = ((f32[8,1,2048]{2,1,0:T(1,128)}), f32[8,1,2048]{2,1,0:T(1,128)S(1)}, u32[]{:S(2)}, u32[]{:S(2)}) async-start(f32[8,1,2048]{2,1,0:T(1,128)} %reshape.104), calls=%async_computation | async-start | bytes 131072 | tf_op jit(solution)/shard_map/all_to_all | solution.py:106
  375.0 50.1 %all-to-all-start.1 = ((f32[8,1,4,32,768]{4,3,2,1,0:T(8,128)}), f32[8,1,4,32,768]{4,3,2,1,0:T(8,128)}, u32[]{:S(2)}, u32[]{:S(2)}) async-start(f32[8,1,4,32,768]{4,3,2,1,0:T(8,128)} %fusion.35), calls=%async_computation.1 | async-start | bytes 6291456 | tf_op jit(solution)/shard_map/all_to_all | solution.py:109
  398.0 30.4 %copy-start.3 = (bf16[4,32,768]{2,1,0:T(8,128)(2,1)S(1)}, bf16[4,32,768]{2,1,0:T(8,128)(2,1)}, u32[]{:S(2)}) copy-start(bf16[4,32,768]{2,1,0:T(8,128)(2,1)} %param.13) | copy-start | bytes 589828
  398.0 30.4 %copy-start.4 = (f32[768]{0:T(1024)S(1)}, f32[768]{0:T(1024)}, u32[]{:S(2)}) copy-start(f32[768]{0:T(1024)} %param.14) | copy-start | bytes 9220
  428.4 2.8 copy-start.5
Sparse Core Ops, SparseCore 0:
  12.5 69.9 all-gather.1
  86.8 153.3 all-reduce.2
